TPU v7x, 128 devices: a whole 4x4x4 slice. The times are simulated.
128 devices in a mesh: ga: 16 (over x, z_hi, core), ba: 8 (over y, z_lo).
Axes of the slice: x: 4, y: 4, z: 4 (z_hi: 2, z_lo: 2; z = z_hi * 2 + z_lo), core: 2. Of those that a mesh axis runs over, the one named last changes fastest.
Arguments:
- psi: float32 [2, 32768, 2048], P(None, 'ga', 'ba'), may hold values from -0.15625 to 0.15625
- dpsi: float32 [2, 32768, 512], P(None, 'ga', 'ba'), may hold values from -6 to 6
- band_weight: float32 [2048], replicated, may hold values from 0.25 to 1
- panel_band: int32 [16], P('ba'), may hold values from 0 to 15, each once
- slab_offset: int32 [16], replicated, may hold values from 0 to 2047
Outputs:
- projected: float32 [2, 32768, 512], P(None, 'ga', 'ba')
Inputs may be any that keep to these rules, and one draw needn't show every extreme that they name: panel_band is a permutation of the panel numbers.
All inputs are finite; a program needn't handle non-finite values.
Results may differ from a plain program's by a relative error of at most 0.00012.
Values sent between devices are 32-bit elements; how exact they have to be, the bound alone decides.
A program may use at most 128 MiB of HBM per device.

v0:
```python
import jax
import jax.numpy as jnp
from jax import lax
from jax.sharding import PartitionSpec as P

PANEL = 128


def split_up(value, dim, count):
    before, after = (value.shape[:dim], value.shape[dim + 1 :])
    return jnp.moveaxis(value.reshape(*before, count, -1, *after), dim, 0)


def edges_of(length, count):
    turn = length // count
    if turn >= 8:
        turn -= turn % 8
    return [turn * k for k in range(1, count)]


def in_order(blocks, dim):
    lengths = list(blocks.shape[1:])
    lengths[dim] *= blocks.shape[0]
    return jnp.moveaxis(blocks, 0, dim).reshape(lengths)


def cut_exchange(value, axis, pieces, split_dim, concat_dim):
    blocks = split_up(value, split_dim, lax.axis_size(axis))
    split_at = max(range(1, max(2, blocks.ndim - 1)), key=lambda d: blocks.shape[d])
    done = []
    for slab in jnp.split(blocks, edges_of(blocks.shape[split_at], pieces), axis=split_at):
        if slab.size:
            done.append(lax.all_to_all(slab, axis, split_axis=0, concat_axis=0, tiled=True))
    return in_order(jnp.concatenate(done, axis=split_at), concat_dim)


def from_everyone(value, axis):
    count = lax.axis_size(axis)
    return lax.all_to_all(
        jnp.broadcast_to(value[None], (count, *value.shape)), axis, 0, 0, tiled=True
    )


def gather_directly(value, axis, dim):
    blocks = from_everyone(value, axis)
    return in_order(blocks, dim)


def tdot(left, right):
    return lax.dot_general(
        left,
        right,
        (((0,), (0,)), ((), ())),
        precision=lax.Precision.HIGHEST,
        preferred_element_type=jnp.float32,
    )


def mdot(left, right):
    return jnp.dot(left, right, precision=lax.Precision.HIGHEST, preferred_element_type=jnp.float32)


def margin_of(waves, columns):
    over_re = tdot(waves[0], columns[0]) + tdot(waves[1], columns[1])
    over_im = tdot(waves[0], columns[1]) - tdot(waves[1], columns[0])
    return jnp.stack([over_re, over_im])


def correct_with(waves, weighted):
    corr_re = mdot(waves[0], weighted[0]) - mdot(waves[1], weighted[1])
    corr_im = mdot(waves[0], weighted[1]) + mdot(waves[1], weighted[0])
    return jnp.stack([corr_re, corr_im])


def weights_for(band_weight, panels):
    table = band_weight.reshape(-1, PANEL)
    onehot = (panels[:, None] == jnp.arange(table.shape[0], dtype=jnp.int32)[None, :]).astype(
        jnp.float32
    )
    return mdot(onehot, table).reshape(-1)


def per_device(psi, dpsi, band_weight, panel_band, slab_offset):
    offset = slab_offset[lax.axis_index("ga")]
    aligned = jnp.roll(dpsi, -offset, axis=1)
    row_waves, row_columns = (
        cut_exchange(psi, "ba", 2, 1, 2),
        cut_exchange(aligned, "ba", 2, 1, 2),
    )
    all_panels = gather_directly(panel_band, "ba", 0)
    full_weight = weights_for(band_weight, all_panels)
    margin = lax.psum(margin_of(row_waves, row_columns), ("ga", "ba"))
    weighted = margin * full_weight[None, :, None]
    row_result = row_columns - correct_with(row_waves, weighted)
    result = lax.all_to_all(row_result, "ba", split_axis=2, concat_axis=1, tiled=True)
    return jnp.roll(result, offset, axis=1)


def solution(mesh):
    in_specs = (P(None, "ga", "ba"), P(None, "ga", "ba"), P(), P("ba"), P())
    out_specs = P(None, "ga", "ba")
    return jax.shard_map(
        per_device, mesh=mesh, in_specs=in_specs, out_specs=out_specs, check_vma=False
    )
```

profile of v0, /device:TPU:2, one launch (start us, length us, event | category | flops | bytes accessed | tf_op | source)
XLA Modules:
  0.0 354.8 jit_solution(3534208202760883374)
XLA Ops:
  6.5 0.0 copy-start
  6.5 1.2 dynamic_slice.6
  8.9 1.8 fusion.9
  10.8 0.3 copy.34
  11.1 0.1 fusion.15
  11.2 0.9 copy.21
  12.1 5.8 %all-to-all-start.1 = ((f32[8,2,128,64]{2,3,1,0:T(8,128)}), f32[8,2,128,64]{2,3,1,0:T(8,128)S(1)}, u32[]{:S(2)}, u32[]{:S(2)}) async-start(f32[8,2,128,64]{2,3,1,0:T(8,128)} %copy.21), calls=%async_computation.1 | async-start | bytes 1048576 | tf_op jit(solution)/shard_map/all_to_all | solution.py:33
  17.9 0.9 copy.20
  18.8 8.7 %all-to-all-done.1 = f32[8,2,128,64]{2,3,1,0:T(8,128)S(1)} async-done(((f32[8,2,128,64]{2,3,1,0:T(8,128)}), f32[8,2,128,64]{2,3,1,0:T(8,128)S(1)}, u32[]{:S(2)}, u32[]{:S(2)}) %all-to-all-start.1) | async-done | bytes 524320 | tf_op jit(solution)/shard_map/all_to_all | solution.py:33
  27.5 3.5 all-to-all-start
  31.0 4.0 %fusion.13 = (f32[8,2,128,256]{3,2,0,1:T(8,128)}, f32[8,2,128,256]{3,2,0,1:T(8,128)S(1)}) fusion(f32[8,2,256,256]{3,2,0,1:T(8,128)} %bitcast.83), kind=kLoop, calls=%fused_computation.29 | loop fusion | bytes 8388608 | tf_op jit(solution)/shard_map/split | solution.py:31
  34.9 1.6 copy.25
  36.5 3.4 all-to-all-done
  39.9 3.6 %all-to-all-start.3 = ((f32[8,2,128,256]{3,2,1,0:T(8,128)}), f32[8,2,128,256]{3,2,1,0:T(8,128)S(1)}, u32[]{:S(2)}, u32[]{:S(2)}) async-start(f32[8,2,128,256]{3,2,1,0:T(8,128)} %copy.25), calls=%async_computation.3 | async-start | bytes 4194304 | tf_op jit(solution)/shard_map/all_to_all | solution.py:33
  43.5 3.1 copy.24
  46.6 26.9 %all-to-all-done.3 = f32[8,2,128,256]{3,2,1,0:T(8,128)S(1)} async-done(((f32[8,2,128,256]{3,2,1,0:T(8,128)}), f32[8,2,128,256]{3,2,1,0:T(8,128)S(1)}, u32[]{:S(2)}, u32[]{:S(2)}) %all-to-all-start.3) | async-done | bytes 2097184 | tf_op jit(solution)/shard_map/all_to_all | solution.py:33
  73.5 4.3 %all-to-all-start.2 = ((f32[8,2,128,256]{3,2,1,0:T(8,128)}), f32[8,2,128,256]{3,2,1,0:T(8,128)}, u32[]{:S(2)}, u32[]{:S(2)}) async-start(f32[8,2,128,256]{3,2,1,0:T(8,128)} %copy.24), calls=%async_computation.2 | async-start | bytes 4194304 | tf_op jit(solution)/shard_map/all_to_all | solution.py:33
  77.8 0.0 all-reduce.2.cloned.1.call-start
  77.9 1.1 copy_bitcast_fusion
  79.0 0.1 fusion.14
  79.1 1.9 copy.27
  81.0 0.0 copy-start.3
  81.0 26.4 %all-to-all-done.2 = f32[8,2,128,256]{3,2,1,0:T(8,128)} async-done(((f32[8,2,128,256]{3,2,1,0:T(8,128)}), f32[8,2,128,256]{3,2,1,0:T(8,128)}, u32[]{:S(2)}, u32[]{:S(2)}) %all-to-all-start.2) | async-done | bytes 2097184 | tf_op jit(solution)/shard_map/all_to_all | solution.py:33
  107.4 3.3 copy.26
  110.7 0.0 copy-done.3
  110.7 2.1 maximum_bitcast_fusion
  112.8 0.4 fusion.12
  113.2 0.0 copy-start.1
  113.2 3.7 %fusion.17 = f32[2048,512]{1,0:T(8,128)S(1)} fusion(f32[256,2048]{0,1:T(8,128)S(1)} %bitcast.68, f32[256,512]{0,1:T(8,128)S(1)} %bitcast.76), kind=kOutput, calls=%fused_computation.33 | convolution fusion | flops 3221225472 | bytes 6815744 | tf_op jit(solution)/shard_map/dot_general | solution.py:50
  116.9 3.7 %fusion.16 = f32[2048,512]{1,0:T(8,128)S(1)} fusion(f32[256,2048]{0,1:T(8,128)S(1)} %bitcast.69, f32[256,512]{0,1:T(8,128)S(1)} %bitcast.78), kind=kOutput, calls=%fused_computation.32 | convolution fusion | flops 3221225472 | bytes 6815744 | tf_op jit(solution)/shard_map/dot_general | solution.py:50
  120.7 3.8 %subtract_bitcast_fusion = f32[1,2048,512]{2,1,0:T(8,128)S(1)} fusion(f32[2048,512]{1,0:T(8,128)S(1)} %fusion.17, f32[256,2048]{0,1:T(8,128)S(1)} %bitcast.72, f32[256,512]{0,1:T(8,128)S(1)} %bitcast.79), kind=kOutput, calls=%fused_computation.5 | convolution fusion | flops 3222274048 | bytes 11010048 | tf_op jit(solution)/shard_map/dot_general | solution.py:50
  124.4 0.0 copy-done.1
  124.4 15.3 %add_bitcast_fusion = f32[1,2048,512]{2,1,0:T(8,128)S(1)} fusion(f32[2048,512]{1,0:T(8,128)S(1)} %fusion.16, f32[256,2048]{0,1:T(8,128)S(1)} %bitcast.73, f32[256,512]{0,1:T(8,128)S(1)} %bitcast.77), kind=kOutput, calls=%fused_computation.6 | convolution fusion | flops 3222274048 | bytes 11010048 | tf_op jit(solution)/shard_map/dot_general | solution.py:50
  139.7 4.2 %pad_maximum_fusion = f32[2,2048,512]{2,1,0:T(8,128)} fusion(f32[1,2048,512]{2,1,0:T(8,128)S(1)} %subtract_bitcast_fusion, f32[1,2048,512]{2,1,0:T(8,128)S(1)} %add_bitcast_fusion), kind=kLoop, calls=%fused_computation | loop fusion | flops 2097152 | bytes 16777216 | tf_op jit(solution)/shard_map/stack | solution.py:66
  143.9 0.0 copy-start.6
  143.9 0.0 copy-start.4
  143.9 0.0 all-reduce.2.cloned.1.call-update
  144.0 0.6 copy-done.6
  144.6 8.5 %all_to_all.44 = s32[8,1,2]{2,1,0:T(1,128)S(1)} all-to-all(s32[8,1,2]{2,1,0:T(1,128)S(1)} %broadcast_in_dim.2), channel_id=1, replica_groups=mesh['ga'=16,'ba'=8] {'ba'}, dimensions={0} | all-to-all | bytes 128 | tf_op jit(solution)/shard_map/all_to_all | solution.py:39
  153.1 0.6 broadcast.7
  153.7 0.7 reduce.3
  154.4 0.1 eq.17
  154.5 0.0 copy-done
  154.5 0.2 convolution_bitcast_fusion
  154.7 0.0 copy-done.4
  154.7 1.3 copy.28
  156.0 148.4 %all-reduce.2.cloned.1.call-done = f32[2,2048,512]{2,1,0:T(8,128)} async-done(((f32[2,2048,512]{2,1,0:T(8,128)}), f32[2,2048,512]{2,1,0:T(8,128)}) %all-reduce.2.cloned.1.call-update) | async-done | bytes 8388624 | tf_op jit(solution)/shard_map/psum | solution.py:92
  304.4 0.0 copy-start.2
  304.4 4.1 %broadcast_multiply_fusion = f32[2,2048,512]{2,1,0:T(8,128)S(1)} fusion(f32[2,2048,512]{2,1,0:T(8,128)} %all-reduce.2.cloned.1.call-done, f32[2048]{0:T(1024)S(1)} %convolution_bitcast_fusion), kind=kLoop, calls=%fused_computation.4 | loop fusion | flops 2097152 | bytes 16785408 | tf_op jit(solution)/shard_map/mul | solution.py:93
  308.6 0.0 copy-done.2
  308.6 3.8 %fusion = f32[256,512]{1,0:T(8,128)S(1)} fusion(f32[256,2048]{0,1:T(8,128)S(1)} %bitcast.74, f32[2,2048,512]{2,1,0:T(8,128)S(1)} %broadcast_multiply_fusion), kind=kOutput, calls=%fused_computation.7 | convolution fusion | flops 3221225472 | bytes 6815744 | tf_op jit(solution)/shard_map/dot_general | solution.py:60
  312.4 3.9 %fusion.1 = f32[256,512]{1,0:T(8,128)S(1)} fusion(f32[256,2048]{0,1:T(8,128)S(1)} %bitcast.70, f32[2,2048,512]{2,1,0:T(8,128)S(1)} %broadcast_multiply_fusion), kind=kOutput, calls=%fused_computation.8 | convolution fusion | flops 3221225472 | bytes 6815744 | tf_op jit(solution)/shard_map/dot_general | solution.py:60
  316.3 4.1 %fusion.7 = f32[1,256,512]{2,1,0:T(8,128)S(1)} fusion(f32[256,512]{1,0:T(8,128)S(1)} %fusion, f32[256,2048]{0,1:T(8,128)S(1)} %bitcast.71, f32[2,2048,512]{2,1,0:T(8,128)S(1)} %broadcast_multiply_fusion), kind=kOutput, calls=%fused_computation.18 | convolution fusion | flops 3221356544 | bytes 7340032 | tf_op jit(solution)/shard_map/dot_general | solution.py:60
  320.3 0.0 copy-start.5
  320.4 3.8 %fusion.5 = f32[1,256,512]{2,1,0:T(8,128)S(1)} fusion(f32[256,512]{1,0:T(8,128)S(1)} %fusion.1, f32[256,2048]{0,1:T(8,128)S(1)} %bitcast.75, f32[2,2048,512]{2,1,0:T(8,128)S(1)} %broadcast_multiply_fusion), kind=kOutput, calls=%fused_computation.16 | convolution fusion | flops 3221356544 | bytes 7340032 | tf_op jit(solution)/shard_map/dot_general | solution.py:60
  324.2 0.0 copy-done.5
  324.2 0.2 maximum_subtract_fusion
  324.4 1.3 copy.29
  325.7 3.6 %all-to-all-start.5 = ((f32[2,256,512]{1,0,2:T(2,128)}), f32[2,256,512]{1,0,2:T(2,128)S(1)}, u32[]{:S(2)}, u32[]{:S(2)}) async-start(f32[2,256,512]{1,0,2:T(2,128)} %copy.29), calls=%async_computation.5 | async-start | bytes 2097152 | tf_op jit(solution)/shard_map/all_to_all | solution.py:95
  330.5 15.5 %all-to-all-done.5 = f32[2,256,512]{1,0,2:T(2,128)S(1)} async-done(((f32[2,256,512]{1,0,2:T(2,128)}), f32[2,256,512]{1,0,2:T(2,128)S(1)}, u32[]{:S(2)}, u32[]{:S(2)}) %all-to-all-start.5) | async-done | bytes 1048608 | tf_op jit(solution)/shard_map/all_to_all | solution.py:95
  346.0 0.1 copy.30
  346.1 0.1 copy.33
  346.2 1.6 fusion.8
  (1 shorter events, 0.0 us)
Async XLA Ops:
  6.5 148.0 %copy-start = (f32[2048]{0:T(1024)S(1)}, f32[2048]{0:T(1024)}, u32[]{:S(2)}) copy-start(f32[2048]{0:T(1024)} %param.9) | copy-start | bytes 24580
  12.1 15.4 %all-to-all-start.1 = ((f32[8,2,128,64]{2,3,1,0:T(8,128)}), f32[8,2,128,64]{2,3,1,0:T(8,128)S(1)}, u32[]{:S(2)}, u32[]{:S(2)}) async-start(f32[8,2,128,64]{2,3,1,0:T(8,128)} %copy.21), calls=%async_computation.1 | async-start | bytes 1048576 | tf_op jit(solution)/shard_map/all_to_all | solution.py:33
  27.5 12.4 %all-to-all-start = ((f32[8,2,128,64]{2,3,1,0:T(8,128)}), f32[8,2,128,64]{2,3,1,0:T(8,128)S(1)}, u32[]{:S(2)}, u32[]{:S(2)}) async-start(f32[8,2,128,64]{2,3,1,0:T(8,128)} %copy.20), calls=%async_computation | async-start | bytes 1048576 | tf_op jit(solution)/shard_map/all_to_all | solution.py:33
  39.9 33.6 %all-to-all-start.3 = ((f32[8,2,128,256]{3,2,1,0:T(8,128)}), f32[8,2,128,256]{3,2,1,0:T(8,128)S(1)}, u32[]{:S(2)}, u32[]{:S(2)}) async-start(f32[8,2,128,256]{3,2,1,0:T(8,128)} %copy.25), calls=%async_computation.3 | async-start | bytes 4194304 | tf_op jit(solution)/shard_map/all_to_all | solution.py:33
  73.5 33.9 %all-to-all-start.2 = ((f32[8,2,128,256]{3,2,1,0:T(8,128)}), f32[8,2,128,256]{3,2,1,0:T(8,128)}, u32[]{:S(2)}, u32[]{:S(2)}) async-start(f32[8,2,128,256]{3,2,1,0:T(8,128)} %copy.24), calls=%async_computation.2 | async-start | bytes 4194304 | tf_op jit(solution)/shard_map/all_to_all | solution.py:33
  77.8 226.6 %all-reduce.2.cloned.1.call-start = ((), (), s32[]{:S(2)}) async-start(), calls=%async_computation.6 | async-start | bytes 16777216 | tf_op jit(solution)/shard_map/psum | solution.py:92
  81.0 29.7 %copy-start.3 = (f32[8,2,128,256]{2,3,0,1:T(8,128)S(1)}, f32[8,2,128,256]{2,3,0,1:T(8,128)}, u32[]{:S(2)}) copy-start(f32[8,2,128,256]{2,3,0,1:T(8,128)} %copy.27) | copy-start | bytes 6291460
  113.2 11.2 %copy-start.1 = (f32[1,256,8,256]{1,3,2,0:T(8,128)}, f32[1,256,8,256]{1,3,2,0:T(8,128)S(1)}, u32[]{:S(2)}) copy-start(f32[1,256,8,256]{1,3,2,0:T(8,128)S(1)} %get-tuple-element.7) | copy-start | bytes 6291460
  143.9 0.7 copy-start.6
  143.9 10.8 %copy-start.4 = (f32[8,2,256,64]{2,3,0,1:T(8,128)S(1)}, f32[8,2,256,64]{2,3,0,1:T(8,128)}, u32[]{:S(2)}) copy-start(f32[8,2,256,64]{2,3,0,1:T(8,128)} %get-tuple-element.13) | copy-start | bytes 3145732
  304.4 4.1 %copy-start.2 = (f32[1,256,8,256]{1,3,2,0:T(8,128)S(1)}, f32[1,256,8,256]{1,3,2,0:T(8,128)}, u32[]{:S(2)}) copy-start(f32[1,256,8,256]{1,3,2,0:T(8,128)} %copy-done.1) | copy-start | bytes 6291460
  320.3 3.9 %copy-start.5 = (f32[2,256,512]{2,1,0:T(8,128)S(1)}, f32[2,256,512]{2,1,0:T(8,128)}, u32[]{:S(2)}) copy-start(f32[2,256,512]{2,1,0:T(8,128)} %copy.28) | copy-start | bytes 3145732
  325.7 20.3 %all-to-all-start.5 = ((f32[2,256,512]{1,0,2:T(2,128)}), f32[2,256,512]{1,0,2:T(2,128)S(1)}, u32[]{:S(2)}, u32[]{:S(2)}) async-start(f32[2,256,512]{1,0,2:T(2,128)} %copy.29), calls=%async_computation.5 | async-start | bytes 2097152 | tf_op jit(solution)/shard_map/all_to_all | solution.py:95
Sparse Core Ops, SparseCore 0:
  144.1 160.2 all-reduce.1
where the time goes:
time: 359 us; the launch traced here: 355 us
  waiting for transfers between devices  229 us (64%)
  matrix products  42.2 us (12%)
  local copies, waits for them, and re-layouts  21.8 us (6%)
  starting transfers between devices  20.9 us (6%)
  between operations  16.2 us (5%)
  other arithmetic  15.9 us (4%)
  blocking collectives  8.52 us (2%)
    psum x1, waiting for transfers between devices, per_device(): margin = lax.psum(margin_of(row_waves, row_columns), ('ga', 'ba'))  148 us
    all_to_all x4, waiting for transfers between devices, cut_exchange(): lax.all_to_all(slab, axis, split_axis=0, concat_axis=0, tiled=True)  65.3 us
    dot_general x4, matrix products, tdot(): lax.dot_general(left, right, (((0,), (0,)), ((), ())), precision=lax.Prec...  26.5 us
    all_to_all x4, starting transfers between devices, cut_exchange(): lax.all_to_all(slab, axis, split_axis=0, concat_axis=0, tiled=True)  17.3 us
    dot_general x5, matrix products, mdot(): jnp.dot(left, right, precision=lax.Precision.HIGHEST, preferred_element_t...  15.8 us
    all_to_all x1, waiting for transfers between devices, per_device(): lax.all_to_all(row_result, 'ba', split_axis=2, concat_axis=1, tiled=True)  15.5 us
    split x6, local copies, waits for them, and re-layouts, cut_exchange(): jnp.split(blocks, edges_of(blocks.shape[split_at], pieces), axis=split_at)  10.5 us
    all_to_all x1, blocking collectives, from_everyone(): lax.all_to_all(jnp.broadcast_to(value[None], (count, *value.shape)), axis...  8.52 us
  transfers between devices with their start and end apart: 6, of which 6 were waited for; matrix products, arithmetic and copies ran while one was open for 4% of the time, Pallas kernels for 0%

commit v1 on v0

--- a/solution.py
+++ b/solution.py
@@ -89,7 +89,7 @@
     )
     all_panels = gather_directly(panel_band, "ba", 0)
     full_weight = weights_for(band_weight, all_panels)
-    margin = lax.psum(margin_of(row_waves, row_columns), ("ga", "ba"))
+    margin = lax.psum(lax.psum(margin_of(row_waves, row_columns), "ga"), "ba")
     weighted = margin * full_weight[None, :, None]
     row_result = row_columns - correct_with(row_waves, weighted)
     result = lax.all_to_all(row_result, "ba", split_axis=2, concat_axis=1, tiled=True)

time: 359 us -> 745 us (2.08)
  waiting for transfers between devices: 229 us -> 610 us
    psum x1 -> x2, waiting for transfers between devices: 148 us -> 530 us  [per_device(): margin = lax.psum(lax.psum(margin_of(row_waves, row_columns), 'ga'), 'ba')]
  transfers between devices with their start and end apart: 6 -> 7, of which waited for: 6 -> 7; matrix products, arithmetic and copies ran while one was open for 4% -> 2% of each run, Pallas kernels for 0% -> 0%
where the time goes in v1:
time: 745 us; the launch traced here: 742 us
  waiting for transfers between devices  610 us (82%)
  matrix products  42.3 us (6%)
  starting transfers between devices  25.5 us (3%)
  local copies, waits for them, and re-layouts  21.8 us (3%)
  between operations  16.2 us (2%)
  other arithmetic  15.9 us (2%)
  blocking collectives  10.3 us (1%)
    psum x2, waiting for transfers between devices, per_device(): margin = lax.psum(lax.psum(margin_of(row_waves, row_columns), 'ga'), 'ba')  530 us
    all_to_all x4, waiting for transfers between devices, cut_exchange(): lax.all_to_all(slab, axis, split_axis=0, concat_axis=0, tiled=True)  65.3 us
    dot_general x4, matrix products, tdot(): lax.dot_general(left, right, (((0,), (0,)), ((), ())), precision=lax.Prec...  26.5 us
    all_to_all x4, starting transfers between devices, cut_exchange(): lax.all_to_all(slab, axis, split_axis=0, concat_axis=0, tiled=True)  17.3 us
    dot_general x5, matrix products, mdot(): jnp.dot(left, right, precision=lax.Precision.HIGHEST, preferred_element_t...  15.8 us
  transfers between devices with their start and end apart: 7, of which 7 were waited for; matrix products, arithmetic and copies ran while one was open for 2% of the time, Pallas kernels for 0%

profile of v1, /device:TPU:2, one launch (start us, length us, event | category | flops | bytes accessed | tf_op | source)
XLA Modules:
  0.0 741.5 jit_solution(5059571646338722396)
XLA Ops:
  6.5 0.0 copy-start
  6.5 1.2 dynamic_slice.6
  8.9 1.8 fusion.9
  10.8 0.3 copy.34
  11.1 0.1 fusion.15
  11.2 0.9 copy.21
  12.1 5.8 all-to-all-start.1
  17.9 0.9 copy.20
  18.8 8.7 %all-to-all-done.1 = f32[8,2,128,64]{2,3,1,0:T(8,128)S(1)} async-done(((f32[8,2,128,64]{2,3,1,0:T(8,128)}), f32[8,2,128,64]{2,3,1,0:T(8,128)S(1)}, u32[]{:S(2)}, u32[]{:S(2)}) %all-to-all-start.1) | async-done | bytes 524320 | tf_op jit(solution)/shard_map/all_to_all | solution.py:33
  27.5 3.5 all-to-all-start
  31.0 4.0 fusion.13
  34.9 1.6 copy.25
  36.5 3.4 all-to-all-done
  39.9 3.6 all-to-all-start.3
  43.5 3.1 copy.24
  46.6 26.9 %all-to-all-done.3 = f32[8,2,128,256]{3,2,1,0:T(8,128)S(1)} async-done(((f32[8,2,128,256]{3,2,1,0:T(8,128)}), f32[8,2,128,256]{3,2,1,0:T(8,128)S(1)}, u32[]{:S(2)}, u32[]{:S(2)}) %all-to-all-start.3) | async-done | bytes 2097184 | tf_op jit(solution)/shard_map/all_to_all | solution.py:33
  73.5 4.3 all-to-all-start.2
  77.8 0.0 all-reduce.3.cloned.1.call-start
  77.9 1.1 copy_bitcast_fusion
  79.0 0.1 fusion.14
  79.1 1.9 copy.27
  81.0 0.0 copy-start.3
  81.0 26.4 %all-to-all-done.2 = f32[8,2,128,256]{3,2,1,0:T(8,128)} async-done(((f32[8,2,128,256]{3,2,1,0:T(8,128)}), f32[8,2,128,256]{3,2,1,0:T(8,128)}, u32[]{:S(2)}, u32[]{:S(2)}) %all-to-all-start.2) | async-done | bytes 2097184 | tf_op jit(solution)/shard_map/all_to_all | solution.py:33
  107.4 3.3 copy.26
  110.7 0.0 copy-done.3
  110.7 2.1 maximum_bitcast_fusion
  112.8 0.4 fusion.12
  113.2 0.0 copy-start.1
  113.2 3.7 fusion.17
  116.9 3.7 fusion.16
  120.7 3.8 subtract_bitcast_fusion
  124.4 0.0 copy-done.1
  124.4 15.3 %add_bitcast_fusion = f32[1,2048,512]{2,1,0:T(8,128)S(1)} fusion(f32[2048,512]{1,0:T(8,128)S(1)} %fusion.16, f32[256,2048]{0,1:T(8,128)S(1)} %bitcast.73, f32[256,512]{0,1:T(8,128)S(1)} %bitcast.77), kind=kOutput, calls=%fused_computation.6 | convolution fusion | flops 3222274048 | bytes 11010048 | tf_op jit(solution)/shard_map/dot_general | solution.py:50
  139.8 4.2 pad_maximum_fusion
  144.0 0.0 all-reduce.3.cloned.1.call-update
  144.0 0.0 all-reduce.5.cloned.1.call-start
  144.1 199.6 %all-reduce.3.cloned.1.call-done = f32[2,2048,512]{2,1,0:T(8,128)} async-done(((f32[2,2048,512]{2,1,0:T(8,128)}), f32[2,2048,512]{2,1,0:T(8,128)}) %all-reduce.3.cloned.1.call-update) | async-done | bytes 8388624 | tf_op jit(solution)/shard_map/psum | solution.py:92
  343.7 0.0 copy-start.6
  343.7 0.0 all-reduce.5.cloned.1.call-update
  343.7 0.6 copy-done.6
  344.3 10.3 %all_to_all.44 = s32[8,1,2]{2,1,0:T(1,128)S(1)} all-to-all(s32[8,1,2]{2,1,0:T(1,128)S(1)} %broadcast_in_dim.2), channel_id=1, replica_groups=mesh['ga'=16,'ba'=8] {'ba'}, dimensions={0} | all-to-all | bytes 128 | tf_op jit(solution)/shard_map/all_to_all | solution.py:39
  354.6 0.6 broadcast.7
  355.2 0.7 reduce.3
  355.9 0.1 eq.17
  356.0 0.0 copy-done
  356.0 0.2 convolution_bitcast_fusion
  356.2 0.0 copy-done.4
  356.2 1.3 copy.28
  357.5 330.0 %all-reduce.5.cloned.1.call-done = f32[2,2048,512]{2,1,0:T(8,128)} async-done(((f32[2,2048,512]{2,1,0:T(8,128)}), f32[2,2048,512]{2,1,0:T(8,128)}) %all-reduce.5.cloned.1.call-update) | async-done | bytes 8388624 | tf_op jit(solution)/shard_map/psum | solution.py:92
  687.5 4.1 broadcast_multiply_fusion
  691.6 0.0 copy-done.2
  691.7 3.8 fusion
  695.5 3.9 fusion.1
  699.4 4.1 fusion.7
  703.4 0.0 copy-start.5
  703.4 3.8 fusion.5
  707.3 0.0 copy-done.5
  707.3 0.2 maximum_subtract_fusion
  707.5 1.3 copy.29
  708.8 8.1 %all-to-all-start.5 = ((f32[2,256,512]{1,0,2:T(2,128)}), f32[2,256,512]{1,0,2:T(2,128)S(1)}, u32[]{:S(2)}, u32[]{:S(2)}) async-start(f32[2,256,512]{1,0,2:T(2,128)} %copy.29), calls=%async_computation.5 | async-start | bytes 2097152 | tf_op jit(solution)/shard_map/all_to_all | solution.py:95
  718.1 14.6 %all-to-all-done.5 = f32[2,256,512]{1,0,2:T(2,128)S(1)} async-done(((f32[2,256,512]{1,0,2:T(2,128)}), f32[2,256,512]{1,0,2:T(2,128)S(1)}, u32[]{:S(2)}, u32[]{:S(2)}) %all-to-all-start.5) | async-done | bytes 1048608 | tf_op jit(solution)/shard_map/all_to_all | solution.py:95
  732.7 0.1 copy.30
  732.8 0.1 copy.33
  732.9 1.6 fusion.8
  (3 shorter events, 0.0 us)
Async XLA Ops:
  6.5 349.4 %copy-start = (f32[2048]{0:T(1024)S(1)}, f32[2048]{0:T(1024)}, u32[]{:S(2)}) copy-start(f32[2048]{0:T(1024)} %param.9) | copy-start | bytes 24580
  12.1 15.4 %all-to-all-start.1 = ((f32[8,2,128,64]{2,3,1,0:T(8,128)}), f32[8,2,128,64]{2,3,1,0:T(8,128)S(1)}, u32[]{:S(2)}, u32[]{:S(2)}) async-start(f32[8,2,128,64]{2,3,1,0:T(8,128)} %copy.21), calls=%async_computation.1 | async-start | bytes 1048576 | tf_op jit(solution)/shard_map/all_to_all | solution.py:33
  27.5 12.4 %all-to-all-start = ((f32[8,2,128,64]{2,3,1,0:T(8,128)}), f32[8,2,128,64]{2,3,1,0:T(8,128)S(1)}, u32[]{:S(2)}, u32[]{:S(2)}) async-start(f32[8,2,128,64]{2,3,1,0:T(8,128)} %copy.20), calls=%async_computation | async-start | bytes 1048576 | tf_op jit(solution)/shard_map/all_to_all | solution.py:33
  39.9 33.6 %all-to-all-start.3 = ((f32[8,2,128,256]{3,2,1,0:T(8,128)}), f32[8,2,128,256]{3,2,1,0:T(8,128)S(1)}, u32[]{:S(2)}, u32[]{:S(2)}) async-start(f32[8,2,128,256]{3,2,1,0:T(8,128)} %copy.25), calls=%async_computation.3 | async-start | bytes 4194304 | tf_op jit(solution)/shard_map/all_to_all | solution.py:33
  73.5 33.9 %all-to-all-start.2 = ((f32[8,2,128,256]{3,2,1,0:T(8,128)}), f32[8,2,128,256]{3,2,1,0:T(8,128)}, u32[]{:S(2)}, u32[]{:S(2)}) async-start(f32[8,2,128,256]{3,2,1,0:T(8,128)} %copy.24), calls=%async_computation.2 | async-start | bytes 4194304 | tf_op jit(solution)/shard_map/all_to_all | solution.py:33
  77.8 265.9 %all-reduce.3.cloned.1.call-start = ((), (), s32[]{:S(2)}) async-start(), calls=%async_computation.6 | async-start | bytes 16777216 | tf_op jit(solution)/shard_map/psum | solution.py:92
  81.0 29.7 %copy-start.3 = (f32[8,2,128,256]{2,3,0,1:T(8,128)S(1)}, f32[8,2,128,256]{2,3,0,1:T(8,128)}, u32[]{:S(2)}) copy-start(f32[8,2,128,256]{2,3,0,1:T(8,128)} %copy.27) | copy-start | bytes 6291460
  113.2 11.2 %copy-start.1 = (f32[1,256,8,256]{1,3,2,0:T(8,128)}, f32[1,256,8,256]{1,3,2,0:T(8,128)S(1)}, u32[]{:S(2)}) copy-start(f32[1,256,8,256]{1,3,2,0:T(8,128)S(1)} %get-tuple-element.7) | copy-start | bytes 6291460
  144.0 543.5 %all-reduce.5.cloned.1.call-start = ((), (), s32[]{:S(2)}) async-start(), calls=%async_computation.7 | async-start | bytes 16777216 | tf_op jit(solution)/shard_map/psum | solution.py:92
  343.7 0.7 copy-start.6
  343.7 12.5 %copy-start.4 = (f32[8,2,256,64]{2,3,0,1:T(8,128)S(1)}, f32[8,2,256,64]{2,3,0,1:T(8,128)}, u32[]{:S(2)}) copy-start(f32[8,2,256,64]{2,3,0,1:T(8,128)} %get-tuple-element.13) | copy-start | bytes 3145732
  687.5 4.1 copy-start.2
  703.4 3.9 copy-start.5
  708.8 23.9 %all-to-all-start.5 = ((f32[2,256,512]{1,0,2:T(2,128)}), f32[2,256,512]{1,0,2:T(2,128)S(1)}, u32[]{:S(2)}, u32[]{:S(2)}) async-start(f32[2,256,512]{1,0,2:T(2,128)} %copy.29), calls=%async_computation.5 | async-start | bytes 2097152 | tf_op jit(solution)/shard_map/all_to_all | solution.py:95
Sparse Core Ops, SparseCore 0:
  144.1 199.5 all-reduce.2
  346.2 341.2 all-reduce.4
